TPU v7x, 32 devices: a whole 2x2x4 slice. The times are simulated.
32 devices in a mesh: gx: 4 (over z), gy: 4 (over y, x), gz: 2 (over core).
Axes of the slice: x: 2, y: 2, z: 4, core: 2. Of those that a mesh axis runs over, the one named last changes fastest.
Arguments:
- panel: float32 [8192, 4096], P(('gx', 'gy', 'gz'))
- treat_start: int32 [8192], P(('gx', 'gy', 'gz')), may hold values from 1024 to 4096
- loading_init: float32 [64, 8192], P(None, ('gx', 'gy', 'gz'))
- factor_init: float32 [64, 4096], P(None, ('gx', 'gy', 'gz'))
- unit_init: float32 [8192], P(('gx', 'gy', 'gz'))
- day_init: float32 [4096], replicated
Outputs:
- loading_out: float32 [64, 8192], P(None, ('gx', 'gy', 'gz'))
- factor_out: float32 [64, 4096], P(None, ('gx', 'gy', 'gz'))
- unit_out: float32 [8192], P(('gx', 'gy', 'gz'))
- day_out: float32 [4096], replicated
Inputs may be any that keep to these rules, and one draw needn't show every extreme that they name: A unit is treated from day treat_start on; 4096 means never treated.
All inputs are finite; a program needn't handle non-finite values.
Results may differ from a plain program's by a relative error of at most 0.0001.
Values sent between devices are 32-bit elements; how exact they have to be, the bound alone decides.
A program may use at most 64 MiB of HBM per device.

v0:
```python
import jax
import jax.numpy as jnp
from jax import lax
from jax.sharding import PartitionSpec as P

SWEEPS = 2
RIDGE = 1.0


def solve_spd(matrix, right):
    lower = jnp.linalg.cholesky(matrix)
    middle = lax.linalg.triangular_solve(lower, right, left_side=True, lower=True)
    return lax.linalg.triangular_solve(lower, middle, left_side=True, lower=True, transpose_a=True)


def contract_first(left, right):
    return lax.dot_general(
        left,
        right,
        (((0,), (0,)), ((), ())),
        precision=lax.Precision.HIGHEST,
        preferred_element_type=jnp.float32,
    )


def contract_last(left, right):
    return lax.dot_general(
        left,
        right,
        (((1,), (1,)), ((), ())),
        precision=lax.Precision.HIGHEST,
        preferred_element_type=jnp.float32,
    )


def body(panel, treat_start, loading_init, factor_init, unit_init, day_init):
    unit_rows, total_days = panel.shape
    devices = lax.axis_size(("gx", "gy", "gz"))
    all_units = unit_rows * devices
    slice_days = factor_init.shape[1]
    rank = loading_init.shape[0]
    ridge_eye = jnp.eye(rank, dtype=jnp.float32) * RIDGE
    observed = lax.broadcasted_iota(jnp.int32, (unit_rows, total_days), 1) < treat_start[:, None]
    loading = loading_init
    unit_eff = unit_init
    day_eff = day_init
    factors = None
    owned_factors = factor_init
    for sweep_index in range(SWEEPS):
        unit_gram = lax.psum(contract_last(loading, loading), ("gx", "gy", "gz"))
        if sweep_index == 0:
            fitted = contract_first(
                loading, lax.all_gather(factor_init, ("gx", "gy", "gz"), axis=1, tiled=True)
            )
        else:
            fitted = contract_first(loading, factors)
        imputed = jnp.where(observed, panel, unit_eff[:, None] + day_eff[None, :] + fitted)
        without = imputed - fitted
        day_part = jnp.sum(without, 0)
        row_sums = jnp.sum(without, 1)
        resid = None
        day_sums = lax.psum(day_part, ("gx", "gy", "gz"))
        grand = jnp.sum(day_sums) / (all_units * total_days)
        day_eff = day_sums / all_units - grand
        unit_eff = row_sums / total_days - grand
        resid = imputed - unit_eff[:, None] - day_eff[None, :]
        payload = jnp.dot(loading, resid, precision=lax.Precision.HIGHEST)
        summed = lax.psum(payload, ("gx", "gy", "gz"))
        factors = solve_spd(unit_gram + ridge_eye, summed)
        owned_factors = lax.dynamic_slice_in_dim(
            factors, lax.axis_index(("gx", "gy", "gz")) * slice_days, slice_days, 1
        )
        factor_gram = jnp.dot(factors, factors.T, precision=lax.Precision.HIGHEST)
        loading = solve_spd(factor_gram + ridge_eye, contract_last(factors, resid))
    return (loading, owned_factors, unit_eff, day_eff)


def solution(mesh):
    return jax.shard_map(
        body,
        mesh=mesh,
        in_specs=(
            P(("gx", "gy", "gz"), None),
            P(("gx", "gy", "gz")),
            P(None, ("gx", "gy", "gz")),
            P(None, ("gx", "gy", "gz")),
            P(("gx", "gy", "gz")),
            P(),
        ),
        out_specs=(
            P(None, ("gx", "gy", "gz")),
            P(None, ("gx", "gy", "gz")),
            P(("gx", "gy", "gz")),
            P(),
        ),
        check_vma=False,
    )
```

profile of v0, /device:TPU:0, one launch (start us, length us, event | category | flops | bytes accessed | tf_op | source)
XLA Modules:
  0.0 507.0 jit_solution(17631101533937465551)
XLA Ops:
  7.2 0.7 all-gather.2.cloned.1.call-update
  8.0 0.2 fusion.41
  8.3 57.7 %all-gather.2.cloned.1.call-done = f32[64,4096]{1,0:T(8,128)} async-done(((f32[64,128]{1,0:T(8,128)}), f32[64,4096]{1,0:T(8,128)}) %all-gather.2.cloned.1.call-update) | async-done | bytes 1048592 | tf_op jit(solution)/shard_map/all_gather | solution.py:53
  65.9 7.9 %subtract_reduce_fusion.3 = (f32[256]{0:T(256)S(1)}, f32[4096]{0:T(1024)S(1)}, f32[256,4096]{1,0:T(8,128)}) fusion(f32[256,4096]{1,0:T(8,128)} %param.15, f32[4096]{0:T(1024)} %param.20, f32[256]{0:T(256)} %param.19, s32[256]{0:T(256)} %param.16, f32[64,256]{1,0:T(8,128)S(1)} %copy-done, f32[64,4096]{1,0:T(8,128)} %all-gather.2.cloned.1.call-done), kind=kOutput, calls=%fused_computation.20 | convolution fusion | flops 812642048 | bytes 9538560 | tf_op jit(solution)/shard_map/dot_general | solution.py:17
  73.8 40.5 %all-reduce.1 = (f32[4096]{0:T(1024)S(1)}, f32[64,64]{0,1:T(8,128)S(1)}) all-reduce(f32[4096]{0:T(1024)S(1)} %get-tuple-element.12, f32[64,64]{0,1:T(8,128)S(1)} %fusion.41), channel_id=1, replica_groups=mesh['gx'=4,'gy'=4,'gz'=2] {'gx','gy','gz'}, use_global_device_ids=true, to_apply=%region_5.0 | all-reduce | flops 8192 | bytes 65536 | tf_op jit(solution)/shard_map/psum | solution.py:62
  114.3 0.6 reduce_sum.56
  115.6 12.0 %convolution_bitcast_fusion = f32[64,4096]{0,1:T(8,128)} fusion(f32[64,256]{1,0:T(8,128)S(1)} %copy-done, f32[4096]{0:T(1024)S(1)} %multiply_subtract_fusion.1, f32[256]{0:T(256)S(1)} %multiply_subtract_fusion.3, f32[256,4096]{1,0:T(8,128)} %param.15, f32[256,4096]{1,0:T(8,128)} %get-tuple-element.17, f32[4096]{0:T(1024)S(1)} %copy-done.3, ...), kind=kOutput, calls=%fused_computation | convolution fusion | flops 811597824 | bytes 9538560 | tf_op jit(solution)/shard_map/dot_general | solution.py:67
  127.6 10.1 %all-reduce.7.cloned.1.call-start = ((), (), s32[]{:S(2)}) async-start(), calls=%async_computation.2 | async-start | bytes 2097152 | tf_op jit(solution)/shard_map/psum | solution.py:68
  137.7 0.1 copy.11
  137.8 5.8 %cholesky.74 = f32[64,64]{1,0:T(8,128)S(1)} custom-call(f32[64,64]{1,0:T(8,128)S(1)} %fusion.34), custom_call_target="Cholesky" | custom-call | tf_op jit(solution)/shard_map/jit(cholesky)/cholesky | solution.py:11
  143.7 0.6 compare_reduce_fusion.3
  144.3 0.7 fusion.11
  145.0 4.9 custom-call.19
  149.9 111.7 %all-reduce.5.cloned.1.call-done = f32[64,4096]{0,1:T(8,128)} async-done(((f32[64,4096]{0,1:T(8,128)}), f32[64,4096]{0,1:T(8,128)}) %all-reduce.5.cloned.1.call-update) | async-done | bytes 1048592 | tf_op jit(solution)/shard_map/psum | solution.py:68
  261.6 4.1 fusion.30
  265.7 1.0 fusion.32
  266.7 1.0 convolution_add_fusion.1
  267.7 6.6 %fusion = f32[64,256]{1,0:T(8,128)S(1)} fusion(f32[64,4096]{1,0:T(8,128)S(1)} %fusion.32, f32[4096]{0:T(1024)S(1)} %multiply_subtract_fusion.1, f32[256]{0:T(256)S(1)} %multiply_subtract_fusion.3, f32[256,4096]{1,0:T(8,128)S(1)} %copy-done.1, f32[256,4096]{1,0:T(8,128)} %get-tuple-element.17, f32[4096]{0:T(1024)S(1)} %copy-done.3, f32[256]{0:T(256)S(1)} %copy-done.6, ...), kind=kOutput, calls=%fused_computation.6 | convolution fusion | flops 811597824 | bytes 9538560 | tf_op jit(solution)/shard_map/dot_general | solution.py:27
  274.3 0.1 copy.13
  274.4 5.8 %cholesky.85 = f32[64,64]{1,0:T(8,128)S(1)} custom-call(f32[64,64]{1,0:T(8,128)S(1)} %fusion.29), custom_call_target="Cholesky" | custom-call | tf_op jit(solution)/shard_map/jit(cholesky)/cholesky | solution.py:11
  280.3 0.6 compare_reduce_fusion.2
  281.0 0.7 fusion.12
  281.6 4.9 custom-call.21
  286.5 0.3 fusion.25
  286.8 0.2 fusion.27
  287.0 7.7 %subtract_reduce_fusion.1 = (f32[256]{0:T(256)S(1)}, f32[4096]{0:T(1024)S(1)}, f32[256,4096]{1,0:T(8,128)}) fusion(f32[256,4096]{1,0:T(8,128)} %param.15, f32[4096]{0:T(1024)S(1)} %multiply_subtract_fusion.1, f32[256]{0:T(256)S(1)} %multiply_subtract_fusion.3, s32[256]{0:T(256)S(1)} %copy-done.5, f32[64,256]{1,0:T(8,128)S(1)} %fusion.27, ...), kind=kOutput, calls=%fused_computation.18 | convolution fusion | flops 812642048 | bytes 9538560 | tf_op jit(solution)/shard_map/dot_general | solution.py:17
  294.7 0.2 fusion.42
  294.9 39.5 %all-reduce = (f32[4096]{0:T(1024)S(1)}, f32[64,64]{0,1:T(8,128)S(1)}) all-reduce(f32[4096]{0:T(1024)S(1)} %get-tuple-element.10, f32[64,64]{0,1:T(8,128)S(1)} %fusion.42), channel_id=1, replica_groups=mesh['gx'=4,'gy'=4,'gz'=2] {'gx','gy','gz'}, use_global_device_ids=true, to_apply=%region_11.17 | all-reduce | flops 8192 | bytes 65536 | tf_op jit(solution)/shard_map/psum | solution.py:62
  334.5 0.1 copy.15
  334.6 0.6 reduce_sum.59
  335.9 8.1 %fusion.2 = f32[64,4096]{1,0:T(8,128)} fusion(f32[64,256]{1,0:T(8,128)S(1)} %fusion.27, f32[4096]{0:T(1024)S(1)} %multiply_subtract_fusion, f32[256]{0:T(256)S(1)} %multiply_subtract_fusion.2, f32[256,4096]{1,0:T(8,128)} %param.15, f32[256,4096]{1,0:T(8,128)} %get-tuple-element.18, f32[4096]{0:T(1024)S(1)} %multiply_subtract_fusion.1, ...), kind=kOutput, calls=%fused_computation.8 | convolution fusion | flops 811597824 | bytes 9538560 | tf_op jit(solution)/shard_map/dot_general | solution.py:67
  344.0 5.8 %cholesky.96 = f32[64,64]{1,0:T(8,128)S(1)} custom-call(f32[64,64]{1,0:T(8,128)S(1)} %fusion.24), custom_call_target="Cholesky" | custom-call | tf_op jit(solution)/shard_map/jit(cholesky)/cholesky | solution.py:11
  349.9 0.6 compare_reduce_fusion.1
  350.5 0.7 fusion.13
  351.2 4.9 custom-call.23
  356.1 119.0 %all-reduce.7.cloned.1.call-done = f32[64,4096]{1,0:T(8,128)} async-done(((f32[64,4096]{1,0:T(8,128)}), f32[64,4096]{1,0:T(8,128)}) %all-reduce.7.cloned.1.call-update) | async-done | bytes 1048592 | tf_op jit(solution)/shard_map/psum | solution.py:68
  475.1 2.4 fusion.20
  477.5 1.0 fusion.22
  478.5 1.0 convolution_add_fusion
  479.5 6.6 %fusion.1 = f32[64,256]{1,0:T(8,128)S(1)} fusion(f32[64,4096]{1,0:T(8,128)S(1)} %fusion.22, f32[4096]{0:T(1024)S(1)} %multiply_subtract_fusion, f32[256]{0:T(256)S(1)} %multiply_subtract_fusion.2, f32[256,4096]{1,0:T(8,128)S(1)} %copy-done.2, f32[256,4096]{1,0:T(8,128)} %get-tuple-element.18, f32[4096]{0:T(1024)S(1)} %multiply_subtract_fusion.1, ...), kind=kOutput, calls=%fused_computation.7 | convolution fusion | flops 811597824 | bytes 9538560 | tf_op jit(solution)/shard_map/dot_general | solution.py:27
  486.2 0.1 copy.17
  486.2 5.8 %cholesky.107 = f32[64,64]{1,0:T(8,128)S(1)} custom-call(f32[64,64]{1,0:T(8,128)S(1)} %fusion.19), custom_call_target="Cholesky" | custom-call | tf_op jit(solution)/shard_map/jit(cholesky)/cholesky | solution.py:11
  492.1 0.6 compare_reduce_fusion
  492.8 0.7 fusion.14
  493.4 4.9 custom-call.25
  498.3 0.3 fusion.15
  498.6 0.8 fusion.17
  499.4 0.6 constant_dynamic-slice_fusion
  (34 shorter events, 0.4 us)
Async XLA Ops:
  7.2 0.8 copy-start
  7.2 58.7 %all-gather.2.cloned.1.call-start = ((), (), s32[]{:S(2)}) async-start(), calls=%async_computation | async-start | bytes 1081344 | tf_op jit(solution)/shard_map/all_gather | solution.py:53
  7.9 253.7 %all-reduce.5.cloned.1.call-start = ((), (), s32[]{:S(2)}) async-start(), calls=%async_computation.1 | async-start | bytes 4194304 | tf_op jit(solution)/shard_map/psum | solution.py:68
  8.2 107.4 %copy-start.3 = (f32[4096]{0:T(1024)S(1)}, f32[4096]{0:T(1024)}, u32[]{:S(2)}) copy-start(f32[4096]{0:T(1024)} %param.20) | copy-start | bytes 49156
  8.2 107.4 %copy-start.5 = (s32[256]{0:T(256)S(1)}, s32[256]{0:T(256)}, u32[]{:S(2)}) copy-start(s32[256]{0:T(256)} %param.16) | copy-start | bytes 3076
  8.2 107.4 %copy-start.6 = (f32[256]{0:T(256)S(1)}, f32[256]{0:T(256)}, u32[]{:S(2)}) copy-start(f32[256]{0:T(256)} %param.19) | copy-start | bytes 3076
  127.6 347.5 %all-reduce.7.cloned.1.call-start = ((), (), s32[]{:S(2)}) async-start(), calls=%async_computation.2 | async-start | bytes 2097152 | tf_op jit(solution)/shard_map/psum | solution.py:68
  261.6 6.1 %copy-start.1 = (f32[256,4096]{1,0:T(8,128)S(1)}, f32[256,4096]{1,0:T(8,128)}, u32[]{:S(2)}) copy-start(f32[256,4096]{1,0:T(8,128)} %param.15) | copy-start | bytes 12582916
  335.8 143.6 %copy-start.4 = (f32[4096]{0:T(1024)}, f32[4096]{0:T(1024)S(1)}, u32[]{:S(2)}) copy-start(f32[4096]{0:T(1024)S(1)} %multiply_subtract_fusion) | copy-start | bytes 49156
  335.9 143.6 %copy-start.7 = (f32[256]{0:T(256)}, f32[256]{0:T(256)S(1)}, u32[]{:S(2)}) copy-start(f32[256]{0:T(256)S(1)} %multiply_subtract_fusion.2) | copy-start | bytes 3076
  475.1 4.4 copy-start.2
Sparse Core Ops, SparseCore 0:
  10.9 55.0 all-gather.1
  127.7 133.8 all-reduce.4
  344.1 130.8 all-reduce.6
where the time goes:
time: 515 us; the launch traced here: 507 us
  waiting for transfers between devices  289 us (56%)
  blocking collectives  80 us (16%)
  matrix products  61.4 us (12%)
  other arithmetic  49.6 us (10%)
  between operations  15.8 us (3%)
  starting transfers between devices  10.2 us (2%)
    psum x2, waiting for transfers between devices, body(): summed = lax.psum(payload, ('gx', 'gy', 'gz'))  231 us
    psum x2, blocking collectives, body(): day_sums = lax.psum(day_part, ('gx', 'gy', 'gz'))  80 us
    all_gather x1, waiting for transfers between devices, body(): lax.all_gather(factor_init, ('gx', 'gy', 'gz'), axis=1, tiled=True)  57.7 us
    another operation x12, other arithmetic, solve_spd(): lower = jnp.linalg.cholesky(matrix)  26.1 us
    another operation x8, other arithmetic, solve_spd(): lax.linalg.triangular_solve(lower, middle, left_side=True, lower=True, tr...  22.2 us
    dot_general x2, matrix products, body(): payload = jnp.dot(loading, resid, precision=lax.Precision.HIGHEST)  20 us
    dot_general x2, matrix products, contract_first(): lax.dot_general(left, right, (((0,), (0,)), ((), ())), precision=lax.Prec...  15.6 us
    dot_general x4, matrix products, contract_last(): lax.dot_general(left, right, (((1,), (1,)), ((), ())), precision=lax.Prec...  13.7 us
  transfers between devices with their start and end apart: 3, of which 3 were waited for; matrix products, arithmetic and copies ran while one was open for 5% of the time, Pallas kernels for 0%

commit v1 on v0

--- a/solution.py
+++ b/solution.py
@@ -5,6 +5,11 @@
 
 SWEEPS = 2
 RIDGE = 1.0
+
+
+def gather_and_add(x, mesh_axis):
+    terms = lax.all_gather(x, mesh_axis)
+    return jnp.sum(terms, axis=0)
 
 
 def solve_spd(matrix, right):
@@ -65,7 +70,7 @@
         unit_eff = row_sums / total_days - grand
         resid = imputed - unit_eff[:, None] - day_eff[None, :]
         payload = jnp.dot(loading, resid, precision=lax.Precision.HIGHEST)
-        summed = lax.psum(payload, ("gx", "gy", "gz"))
+        summed = gather_and_add(payload, ("gx", "gy", "gz"))
         factors = solve_spd(unit_gram + ridge_eye, summed)
         owned_factors = lax.dynamic_slice_in_dim(
             factors, lax.axis_index(("gx", "gy", "gz")) * slice_days, slice_days, 1

time: 515 us -> 646 us (1.25); the launches traced: 507 us -> 645 us
  waiting for transfers between devices: 289 us -> 423 us
  other arithmetic: 49.6 us -> 73.3 us
  starting transfers between devices: 10.2 us -> 0.12 us
  matrix products: 61.4 us -> 53.2 us
    all_gather x0 -> x2, waiting for transfers between devices: none -> 364 us  [gather_and_add(): terms = lax.all_gather(x, mesh_axis)]
    psum x2 -> x0, waiting for transfers between devices: 231 us -> none  [body(): summed = lax.psum(payload, ('gx', 'gy', 'gz'))]
    reduce_sum x0 -> x2, other arithmetic: none -> 23.7 us  [gather_and_add(): return jnp.sum(terms, axis=0)]
    psum x2 -> x0, starting transfers between devices: 10.1 us -> none  [body(): summed = lax.psum(payload, ('gx', 'gy', 'gz'))]
  transfers between devices with their start and end apart: 3 -> 3, of which waited for: 3 -> 3; matrix products, arithmetic and copies ran while one was open for 5% -> 4% of each run, Pallas kernels for 0% -> 0%
where the time goes in v1:
time: 646 us; the launch traced here: 645 us
  waiting for transfers between devices  423 us (65%)
  blocking collectives  79.4 us (12%)
  other arithmetic  73.3 us (11%)
  matrix products  53.2 us (8%)
  between operations  15.4 us (2%)
    all_gather x2, waiting for transfers between devices, gather_and_add(): terms = lax.all_gather(x, mesh_axis)  364 us
    psum x2, blocking collectives, body(): day_sums = lax.psum(day_part, ('gx', 'gy', 'gz'))  79.4 us
    all_gather x1, waiting for transfers between devices, body(): lax.all_gather(factor_init, ('gx', 'gy', 'gz'), axis=1, tiled=True)  57.7 us
    another operation x12, other arithmetic, solve_spd(): lower = jnp.linalg.cholesky(matrix)  26.1 us
    reduce_sum x2, other arithmetic, gather_and_add(): return jnp.sum(terms, axis=0)  23.7 us
    another operation x8, other arithmetic, solve_spd(): lax.linalg.triangular_solve(lower, middle, left_side=True, lower=True, tr...  22.2 us
    dot_general x2, matrix products, body(): payload = jnp.dot(loading, resid, precision=lax.Precision.HIGHEST)  16.2 us
    dot_general x2, matrix products, contract_first(): lax.dot_general(left, right, (((0,), (0,)), ((), ())), precision=lax.Prec...  15.7 us
  transfers between devices with their start and end apart: 3, of which 3 were waited for; matrix products, arithmetic and copies ran while one was open for 4% of the time, Pallas kernels for 0%

profile of v1, /device:TPU:0, one launch (start us, length us, event | category | flops | bytes accessed | tf_op | source)
XLA Modules:
  0.0 645.1 jit_solution(2071144809108555544)
XLA Ops:
  7.2 0.7 all-gather.6.cloned.1.call-update
  8.0 0.2 fusion.41
  8.3 57.7 %all-gather.6.cloned.1.call-done = f32[64,4096]{1,0:T(8,128)} async-done(((f32[64,128]{1,0:T(8,128)}), f32[64,4096]{1,0:T(8,128)}) %all-gather.6.cloned.1.call-update) | async-done | bytes 1048592 | tf_op jit(solution)/shard_map/all_gather | solution.py:58
  65.9 8.0 %subtract_reduce_fusion.3 = (f32[256]{0:T(256)S(1)}, f32[4096]{0:T(1024)S(1)}, f32[256,4096]{1,0:T(8,128)}) fusion(f32[256,4096]{1,0:T(8,128)} %param.15, f32[4096]{0:T(1024)} %param.20, f32[256]{0:T(256)} %param.19, s32[256]{0:T(256)} %param.16, f32[64,256]{1,0:T(8,128)S(1)} %copy-done, f32[64,4096]{1,0:T(8,128)} %all-gather.6.cloned.1.call-done), kind=kOutput, calls=%fused_computation.20 | convolution fusion | flops 812642048 | bytes 9538560 | tf_op jit(solution)/shard_map/dot_general | solution.py:22
  73.9 40.4 %all-reduce.1 = (f32[4096]{0:T(1024)S(1)}, f32[64,64]{0,1:T(8,128)S(1)}) all-reduce(f32[4096]{0:T(1024)S(1)} %get-tuple-element.12, f32[64,64]{0,1:T(8,128)S(1)} %fusion.41), channel_id=1, replica_groups=mesh['gx'=4,'gy'=4,'gz'=2] {'gx','gy','gz'}, use_global_device_ids=true, to_apply=%region_5.0 | all-reduce | flops 8192 | bytes 65536 | tf_op jit(solution)/shard_map/psum | solution.py:67
  114.3 0.6 reduce_sum.74
  115.7 8.2 %convolution_bitcast_fusion = f32[64,4096]{1,0:T(8,128)} fusion(f32[64,256]{1,0:T(8,128)S(1)} %copy-done, f32[4096]{0:T(1024)S(1)} %multiply_subtract_fusion.1, f32[256]{0:T(256)S(1)} %multiply_subtract_fusion.3, f32[256,4096]{1,0:T(8,128)} %param.15, f32[256,4096]{1,0:T(8,128)} %get-tuple-element.17, f32[4096]{0:T(1024)S(1)} %copy-done.4, ...), kind=kOutput, calls=%fused_computation | convolution fusion | flops 811597824 | bytes 9538560 | tf_op jit(solution)/shard_map/dot_general | solution.py:72
  124.0 0.1 copy.11
  124.1 5.8 cholesky.74
  129.9 0.6 compare_reduce_fusion.3
  130.6 0.7 fusion.11
  131.3 4.9 custom-call.19
  136.1 181.2 %all-gather.8.cloned.1.call-done = f32[2048,4096]{1,0:T(8,128)} async-done(((f32[64,4096]{1,0:T(8,128)}), f32[2048,4096]{1,0:T(8,128)}) %all-gather.8.cloned.1.call-update) | async-done | bytes 33554448 | tf_op jit(solution)/shard_map/all_gather | solution.py:11
  317.4 11.8 %reduce_sum.75 = f32[64,4096]{1,0:T(8,128)S(1)} reduce(f32[32,64,4096]{2,1,0:T(8,128)} %bitcast.81, f32[]{:T(128)} %constant.62.clone.1), dimensions={0}, to_apply=%region_7.9 | reduce | flops 8126464 | bytes 34603012 | tf_op jit(solution)/shard_map/reduce_sum | solution.py:12
  329.2 1.0 fusion.30
  330.3 1.0 fusion.32
  331.3 1.0 convolution_add_fusion.1
  332.3 6.6 %fusion = f32[64,256]{1,0:T(8,128)S(1)} fusion(f32[64,4096]{1,0:T(8,128)S(1)} %fusion.32, f32[4096]{0:T(1024)S(1)} %multiply_subtract_fusion.1, f32[256]{0:T(256)S(1)} %multiply_subtract_fusion.3, f32[256,4096]{1,0:T(8,128)S(1)} %copy-done.2, f32[256,4096]{1,0:T(8,128)} %get-tuple-element.17, f32[4096]{0:T(1024)S(1)} %copy-done.4, f32[256]{0:T(256)S(1)} %copy-done.7, ...), kind=kOutput, calls=%fused_computation.6 | convolution fusion | flops 811597824 | bytes 9538560 | tf_op jit(solution)/shard_map/dot_general | solution.py:32
  339.0 0.1 copy.13
  339.1 5.8 cholesky.85
  344.9 0.6 compare_reduce_fusion.2
  345.6 0.7 fusion.12
  346.2 4.9 custom-call.21
  351.1 0.3 fusion.25
  351.4 0.2 fusion.27
  351.6 7.7 %subtract_reduce_fusion.1 = (f32[256]{0:T(256)S(1)}, f32[4096]{0:T(1024)S(1)}, f32[256,4096]{1,0:T(8,128)}) fusion(f32[256,4096]{1,0:T(8,128)} %param.15, f32[4096]{0:T(1024)S(1)} %multiply_subtract_fusion.1, f32[256]{0:T(256)S(1)} %multiply_subtract_fusion.3, s32[256]{0:T(256)S(1)} %copy-done.6, f32[64,256]{1,0:T(8,128)S(1)} %fusion.27, ...), kind=kOutput, calls=%fused_computation.18 | convolution fusion | flops 812642048 | bytes 9538560 | tf_op jit(solution)/shard_map/dot_general | solution.py:22
  359.3 0.2 fusion.42
  359.5 39.0 %all-reduce = (f32[4096]{0:T(1024)S(1)}, f32[64,64]{0,1:T(8,128)S(1)}) all-reduce(f32[4096]{0:T(1024)S(1)} %get-tuple-element.10, f32[64,64]{0,1:T(8,128)S(1)} %fusion.42), channel_id=1, replica_groups=mesh['gx'=4,'gy'=4,'gz'=2] {'gx','gy','gz'}, use_global_device_ids=true, to_apply=%region_11.17 | all-reduce | flops 8192 | bytes 65536 | tf_op jit(solution)/shard_map/psum | solution.py:67
  398.5 0.6 reduce_sum.78
  399.8 8.0 %fusion.2 = f32[64,4096]{1,0:T(8,128)} fusion(f32[64,256]{1,0:T(8,128)S(1)} %fusion.27, f32[4096]{0:T(1024)S(1)} %multiply_subtract_fusion, f32[256]{0:T(256)S(1)} %multiply_subtract_fusion.2, f32[256,4096]{1,0:T(8,128)} %param.15, f32[256,4096]{1,0:T(8,128)} %get-tuple-element.18, f32[4096]{0:T(1024)S(1)} %multiply_subtract_fusion.1, ...), kind=kOutput, calls=%fused_computation.8 | convolution fusion | flops 811597824 | bytes 9538560 | tf_op jit(solution)/shard_map/dot_general | solution.py:72
  407.9 0.1 copy.15
  408.0 5.8 cholesky.96
  413.9 0.6 compare_reduce_fusion.1
  414.5 0.7 fusion.13
  415.2 4.9 custom-call.23
  420.1 182.9 %all-gather.10.cloned.1.call-done = f32[2048,4096]{1,0:T(8,128)} async-done(((f32[64,4096]{1,0:T(8,128)}), f32[2048,4096]{1,0:T(8,128)}) %all-gather.10.cloned.1.call-update) | async-done | bytes 33554448 | tf_op jit(solution)/shard_map/all_gather | solution.py:11
  603.0 11.9 %reduce_sum.79 = f32[64,4096]{1,0:T(8,128)S(1)} reduce(f32[32,64,4096]{2,1,0:T(8,128)} %bitcast.80, f32[]{:T(128)} %constant.62.clone.1), dimensions={0}, to_apply=%region_13.19 | reduce | flops 8126464 | bytes 34603012 | tf_op jit(solution)/shard_map/reduce_sum | solution.py:12
  614.9 1.0 fusion.20
  615.9 1.0 fusion.22
  617.0 1.0 convolution_add_fusion
  618.0 6.6 %fusion.1 = f32[64,256]{1,0:T(8,128)S(1)} fusion(f32[64,4096]{1,0:T(8,128)S(1)} %fusion.22, f32[4096]{0:T(1024)S(1)} %multiply_subtract_fusion, f32[256]{0:T(256)S(1)} %multiply_subtract_fusion.2, f32[256,4096]{1,0:T(8,128)S(1)} %copy-done.3, f32[256,4096]{1,0:T(8,128)} %get-tuple-element.18, f32[4096]{0:T(1024)S(1)} %multiply_subtract_fusion.1, ...), kind=kOutput, calls=%fused_computation.7 | convolution fusion | flops 811597824 | bytes 9538560 | tf_op jit(solution)/shard_map/dot_general | solution.py:32
  624.7 5.8 cholesky.107
  630.6 0.6 compare_reduce_fusion
  631.2 0.7 fusion.14
  631.9 4.9 custom-call.25
  636.8 0.3 fusion.15
  637.1 0.8 fusion.17
  637.9 0.6 constant_dynamic-slice_fusion
  (38 shorter events, 0.6 us)
Async XLA Ops:
  7.2 0.8 copy-start
  7.2 58.7 %all-gather.6.cloned.1.call-start = ((), (), s32[]{:S(2)}) async-start(), calls=%async_computation | async-start | bytes 1081344 | tf_op jit(solution)/shard_map/all_gather | solution.py:58
  7.9 309.5 %all-gather.8.cloned.1.call-start = ((), (), s32[]{:S(2)}) async-start(), calls=%async_computation.1 | async-start | bytes 34603008 | tf_op jit(solution)/shard_map/all_gather | solution.py:11
  8.2 107.4 %copy-start.4 = (f32[4096]{0:T(1024)S(1)}, f32[4096]{0:T(1024)}, u32[]{:S(2)}) copy-start(f32[4096]{0:T(1024)} %param.20) | copy-start | bytes 49156
  8.2 107.4 %copy-start.6 = (s32[256]{0:T(256)S(1)}, s32[256]{0:T(256)}, u32[]{:S(2)}) copy-start(s32[256]{0:T(256)} %param.16) | copy-start | bytes 3076
  8.2 107.4 %copy-start.7 = (f32[256]{0:T(256)S(1)}, f32[256]{0:T(256)}, u32[]{:S(2)}) copy-start(f32[256]{0:T(256)} %param.19) | copy-start | bytes 3076
  123.9 479.1 %all-gather.10.cloned.1.call-start = ((), (), s32[]{:S(2)}) async-start(), calls=%async_computation.2 | async-start | bytes 34603008 | tf_op jit(solution)/shard_map/all_gather | solution.py:11
  329.2 3.1 copy-start.2
  399.8 218.2 %copy-start.5 = (f32[4096]{0:T(1024)}, f32[4096]{0:T(1024)S(1)}, u32[]{:S(2)}) copy-start(f32[4096]{0:T(1024)S(1)} %multiply_subtract_fusion) | copy-start | bytes 49156
  399.8 218.2 %copy-start.8 = (f32[256]{0:T(256)}, f32[256]{0:T(256)S(1)}, u32[]{:S(2)}) copy-start(f32[256]{0:T(256)S(1)} %multiply_subtract_fusion.2) | copy-start | bytes 3076
  614.9 3.1 copy-start.3
  616.9 21.6 %copy-start.1 = (f32[64,256]{1,0:T(8,128)S(1)}, f32[64,256]{1,0:T(8,128)}, u32[]{:S(2)}) copy-start(f32[64,256]{1,0:T(8,128)} %param.17) | copy-start | bytes 196612
Sparse Core Ops, SparseCore 0:
  10.9 55.0 all-gather.5
  124.0 193.3 all-gather.7
  408.0 194.9 all-gather.9
